TPU v7x, 128 devices: a whole 4x4x4 slice. The times are simulated.
128 devices in a mesh: data: 1, model: 2 (over core), seq: 64 (over z, y, x).
Axes of the slice: x: 4, y: 4, z: 4, core: 2. Of those that a mesh axis runs over, the one named last changes fastest.
Arguments:
- tokens: bfloat16 [8, 98304, 384], P('data', 'seq')
- lengths: int32 [8], P('data')
- slot_params: bfloat16 [384, 128], replicated
- logit_scale: float32 [], replicated
- w_in: bfloat16 [128, 384, 1536], P('seq', None, 'model')
- w_out: bfloat16 [128, 1536, 384], P('seq', 'model')
Outputs:
- output: bfloat16 [8, 98304, 384], P('data', 'seq')
All inputs are finite; a program needn't handle non-finite values.
Results may differ from a plain program's by a relative error of at most 0.0163054.
Values are sent between devices in bfloat16 or wider.
A program may use at most 1 GiB of HBM per device.

v0:
```python
import jax
import jax.numpy as jnp
from jax import lax
from jax.sharding import PartitionSpec as P

NORM_EPS = 1e-6


def unit_vectors(values, axis):
    v32 = values.astype(jnp.float32)
    return (v32 * lax.rsqrt(jnp.sum(v32 * v32, axis=axis, keepdims=True) + NORM_EPS)).astype(jnp.bfloat16)


def solution(mesh):
    seq_size = mesh.shape["seq"]

    def local_layer(tokens, lengths, slot_params, logit_scale, w_in, w_out):
        batch_size, tok_count, model_dim = tokens.shape
        n_slots = slot_params.shape[1]
        local_experts = w_in.shape[0]
        local_slots = n_slots // seq_size
        slot_per = local_slots // local_experts
        positions = lax.axis_index("seq") * tok_count + jnp.arange(tok_count)
        is_valid = positions[None, :] < lengths[:, None]
        logits = logit_scale * jnp.einsum("bmd,dn->bmn", unit_vectors(tokens, 2), unit_vectors(slot_params, 0), preferred_element_type=jnp.float32)
        masked = jnp.where(is_valid[:, :, None], logits, -1e30)
        col_max = lax.pmax(jnp.max(masked, axis=1, keepdims=True), "seq")
        weights = jnp.exp(masked - col_max)
        col_sum = lax.psum_scatter(jnp.sum(weights, axis=1), "seq", scatter_dimension=1, tiled=True)
        part_sum = jnp.einsum("bmn,bmd->bnd", weights.astype(jnp.bfloat16), tokens, preferred_element_type=jnp.float32)
        slot_sum = lax.psum_scatter(part_sum.astype(jnp.bfloat16), "seq", scatter_dimension=1, tiled=True)
        slot_in = (slot_sum.astype(jnp.float32) / col_sum[:, :, None]).astype(jnp.bfloat16)
        grouped = slot_in.reshape(batch_size, local_experts, slot_per, model_dim)
        hidden = jnp.einsum("besd,edf->besf", grouped, w_in, preferred_element_type=jnp.float32)
        hidden = jax.nn.gelu(hidden, approximate=False).astype(jnp.bfloat16)
        out_part = jnp.einsum("besf,efd->besd", hidden, w_out, preferred_element_type=jnp.float32)
        slot_out = lax.psum(out_part, "model").astype(jnp.bfloat16).reshape(batch_size, local_slots, model_dim)
        all_slots = lax.all_gather(slot_out, "seq", axis=1, tiled=True)
        mix_weights = jax.nn.softmax(logits, axis=-1).astype(jnp.bfloat16)
        mixed = jnp.einsum("bmn,bnd->bmd", mix_weights, all_slots, preferred_element_type=jnp.float32)
        return jnp.where(is_valid[:, :, None], mixed, 0.0).astype(jnp.bfloat16)

    return jax.shard_map(local_layer, mesh=mesh, in_specs=(P("data", "seq", None), P("data"), P(), P(), P("seq", None, "model"), P("seq", "model", None)), out_specs=P("data", "seq", None), check_vma=False)
```

profile of v0, /device:TPU:2, one launch (start us, length us, event | category | flops | bytes accessed | tf_op | source)
XLA Modules:
  0.0 779.6 jit_solution(5433471469477208740)
XLA Ops:
  6.5 0.0 copy-start
  6.5 0.0 copy-start.3
  6.5 0.0 copy-start.4
  6.5 0.0 reduce-scatter.2.cloned.1.call-start
  7.3 1.0 fusion.23
  8.3 0.0 copy-start.1
  8.3 5.8 fusion.1
  14.1 0.0 copy-done.4
  14.1 0.1 broadcast_compare_fusion
  14.2 0.0 copy-done.3
  14.2 0.4 copy-done.1
  14.6 8.1 %select_reduce_fusion = (f32[8,128]{1,0:T(8,128)S(1)}, f32[8,1536,128]{2,1,0:T(8,128)}) fusion(f32[]{:T(128)S(6)} %copy.18, pred[8,1536]{1,0:T(8,128)(4,1)S(1)} %broadcast_compare_fusion, bf16[384,128]{1,0:T(8,128)(2,1)S(1)} %copy-done.3, f32[128]{0:T(128)S(1)} %add_rsqrt_fusion.1, bf16[8,1536,384]{2,1,0:T(8,128)(2,1)S(1)} %copy-done.1, ...), kind=kOutput, calls=%fused_computation.11 | convolution fusion | flops 1226980352 | bytes 15892996 | tf_op jit(solution)/shard_map/bmd,dn->bmn/dot_general | solution.py:25
  22.7 174.3 %pmax.7 = f32[8,128]{1,0:T(8,128)S(1)} all-reduce(f32[8,128]{1,0:T(8,128)S(1)} %get-tuple-element.5), channel_id=1, replica_groups=mesh['data'=1,'model'=2,'seq'=64] {'seq'}, use_global_device_ids=true, to_apply=%region_5.6 | all-reduce | flops 1024 | bytes 8192 | tf_op jit(solution)/shard_map/pmax | solution.py:27
  197.0 7.9 %fusion.9 = bf16[8,128,384]{2,1,0:T(8,128)(2,1)S(1)} fusion(bf16[8,1536,384]{2,1,0:T(8,128)(2,1)} %param.6, f32[8,1536,128]{2,1,0:T(8,128)} %get-tuple-element.6, f32[8,128]{1,0:T(8,128)S(1)} %pmax.7, f32[]{:T(128)S(6)} %copy.18, pred[8,1536]{1,0:T(8,128)(4,1)S(1)} %broadcast_compare_fusion), kind=kOutput, calls=%fused_computation.16 | convolution fusion | flops 1214251008 | bytes 16531460 | tf_op jit(solution)/shard_map/bmn,bmd->bnd/dot_general | solution.py:30
  205.0 0.0 copy-start.5
  205.0 1.3 copy.17
  206.3 0.0 reduce-scatter.2.cloned.1.call-update
  206.3 0.0 copy-start.2
  206.4 6.3 fusion.6
  212.6 0.1 copy.8
  212.7 0.0 copy-done.5
  212.7 0.6 dynamic-slice
  214.0 342.7 %all-reduce = f32[8,128]{0,1:T(8,128)S(1)} all-reduce(f32[8,128]{0,1:T(8,128)S(1)} %copy.8), channel_id=4, replica_groups=mesh['data'=1,'model'=2,'seq'=64] {'seq'}, use_global_device_ids=true, to_apply=%region_8.9.clone | all-reduce | flops 1024 | bytes 8192
  556.7 6.1 fusion.108
  562.8 0.0 reduce-scatter.2.cloned.1.call-done
  562.8 0.0 copy-done
  562.8 0.0 copy-done.2
  562.8 1.2 convolution_bitcast_fusion
  564.0 3.4 psum.7
  567.5 179.0 %all-gather = bf16[8,128,1,384]{3,0,2,1:T(8,128)(2,1)S(1)} all-gather(bf16[8,2,1,384]{3,0,2,1:T(8,128)(2,1)S(1)} %bitcast.89), channel_id=2, replica_groups=mesh['data'=1,'model'=2,'seq'=64] {'seq'}, dimensions={1}, use_global_device_ids=true | all-gather | bytes 798720 | tf_op jit(solution)/shard_map/all_gather | solution.py:38
  746.5 26.2 %select_convert_fusion = bf16[8,1536,384]{2,1,0:T(8,128)(2,1)} fusion(pred[8,1536]{1,0:T(8,128)(4,1)S(1)} %broadcast_compare_fusion, f32[8,1536]{1,0:T(8,128)S(1)} %fusion.108, bf16[8,128,1,384]{3,0,2,1:T(8,128)(2,1)S(1)} %all-gather, f32[8,1536,128]{2,1,0:T(8,128)} %get-tuple-element.6, f32[]{:T(128)S(6)} %copy.18), kind=kOutput, calls=%fused_computation.5 | convolution fusion | flops 1223700608 | bytes 16576516 | tf_op jit(solution)/shard_map/bmn,bnd->bmd/dot_general | solution.py:40
  (4 shorter events, 0.0 us)
Async XLA Ops:
  6.5 556.3 %copy-start = (bf16[2,768,384]{2,1,0:T(8,128)(2,1)S(1)}, bf16[2,768,384]{2,1,0:T(8,128)(2,1)}, u32[]{:S(2)}) copy-start(bf16[2,768,384]{2,1,0:T(8,128)(2,1)} %param.11) | copy-start | bytes 3538948
  6.5 7.7 copy-start.3
  6.5 7.6 copy-start.4
  6.5 556.3 %reduce-scatter.2.cloned.1.call-start = ((), (), s32[]{:S(2)}) async-start(), calls=%async_computation.1 | async-start | bytes 798720 | tf_op jit(solution)/shard_map/reduce_scatter | solution.py:31
  8.3 6.4 copy-start.1
  205.0 7.8 copy-start.5
  206.3 356.5 %copy-start.2 = (bf16[2,384,768]{2,1,0:T(8,128)(2,1)S(1)}, bf16[2,384,768]{2,1,0:T(8,128)(2,1)}, u32[]{:S(2)}) copy-start(bf16[2,384,768]{2,1,0:T(8,128)(2,1)} %param.10) | copy-start | bytes 3538948
Sparse Core Ops, SparseCore 0:
  206.5 221.0 reduce-scatter.1
where the time goes:
time: 780 us
  blocking collectives  699 us (90%)
  matrix products  43.5 us (6%)
  other arithmetic  19.2 us (2%)
  between operations  14.9 us (2%)
    unnamed x1, blocking collectives  343 us
    all_gather x1, blocking collectives, local_layer(): all_slots = lax.all_gather(slot_out, 'seq', axis=1, tiled=True)  179 us
    pmax x1, blocking collectives, local_layer(): col_max = lax.pmax(jnp.max(masked, axis=1, keepdims=True), 'seq')  174 us
    dot_general x1, matrix products, local_layer(): jnp.einsum('bmn,bnd->bmd', mix_weights, all_slots, preferred_element_type...  26.2 us
  transfers between devices with their start and end apart: 1, of which 0 were waited for; matrix products, arithmetic and copies ran while one was open for 2% of the time, Pallas kernels for 0%

commit v1 on v0

v1 whole, which is shorter than its diff:
```python
import functools

import jax
import jax.numpy as jnp
from jax import lax
from jax.experimental import pallas as pl
from jax.experimental.pallas import tpu as pltpu
from jax.sharding import PartitionSpec as P

NORM_EPS = 1e-6
MESH = pl.DeviceIdType.MESH
SIDE = 4
F32, BF16 = jnp.float32, jnp.bfloat16
NEG = -1e30


def dot(a, b, ca, cb):
    return lax.dot_general(a, b, (((ca,), (cb,)), ((), ())), preferred_element_type=F32)


def moe_kernel(lens, scale, phi, x_hbm, win_hbm, wout_hbm, c_hbm, slots_hbm,
               x_v, win_v, wout_v, c_v, u_v, v_v, vt_v, tmp_v, lt_v, w_v, pack_v, send_v, recv_v,
               xs_v, part_v, peer_v, ys_v, ag_v, unpack_v, slots_v,
               x_sem, w_sem, c_sem, s_sem, sems):
    n_batch, toks, dim = x_hbm.shape
    half = n_batch // 2
    slots = phi.shape[1]
    chips = slots // 2
    core = lax.axis_index("model")
    chip = lax.axis_index("seq")
    cz, cy, cx = chip // (SIDE * SIDE), (chip // SIDE) % SIDE, chip % SIDE
    first = core * half
    other = 1 - core

    def batch_of(q):
        return lax.rem(first + q, n_batch)

    def x_copy(q):
        return pltpu.make_async_copy(x_hbm.at[batch_of(q)], x_v.at[q], x_sem.at[q])

    for q in range(n_batch):
        x_copy(q).start()
    win_copy = pltpu.make_async_copy(win_hbm, win_v, w_sem.at[0])
    wout_copy = pltpu.make_async_copy(wout_hbm, wout_v, w_sem.at[1])
    win_copy.start()
    wout_copy.start()

    def peer(r):
        dz, dy, dx = r // (SIDE * SIDE), (r // SIDE) % SIDE, r % SIDE
        return ((cz + dz) % SIDE) * (SIDE * SIDE) + ((cy + dy) % SIDE) * SIDE + (cx + dx) % SIDE

    barrier = pltpu.get_barrier_semaphore()
    pl.semaphore_signal(barrier, inc=1, device_id={"model": other}, device_id_type=MESH)

    @pl.loop(1, chips)
    def _(r):
        pl.semaphore_signal(barrier, inc=1, device_id={"seq": peer(r)}, device_id_type=MESH)

    g = scale[0]

    p32 = phi[...].astype(F32)
    unit = (p32 * lax.rsqrt(jnp.sum(p32 * p32, axis=0, keepdims=True) + NORM_EPS))
    for d in range(dim // 128):
        cols = slice(d * 128, (d + 1) * 128)
        tmp_v[d] = unit[cols, :].T
        for k in range(2):
            vt_v[k * chips:(k + 1) * chips, cols] = tmp_v[d, pl.ds(k, chips, stride=2), :].astype(BF16)
    v_v[...] = vt_v[...].astype(F32).T.astype(BF16)

    rows = 256

    def unit_rows(q):
        for t in range(toks // rows):
            part = x_v[q, t * rows:(t + 1) * rows, :].astype(F32)
            norm = lax.rsqrt(jnp.sum(part * part, axis=1, keepdims=True) + NORM_EPS)
            u_v[t * rows:(t + 1) * rows, :] = (part * norm).astype(BF16)

    lane = lax.broadcasted_iota(jnp.int32, (slots, 128), 1)

    @pl.loop(0, half)
    def _(q):
        x_copy(q).wait()
        unit_rows(q)
        left = lens[batch_of(q)] - chip * toks
        top = jnp.full((slots, rows), NEG, F32)
        for t in range(toks // rows):
            span = slice(t * rows, (t + 1) * rows)
            lg = g * dot(vt_v[...], u_v[span, :], 1, 1)
            pos = lax.broadcasted_iota(jnp.int32, lg.shape, 1) + t * rows
            lg = jnp.where(pos < left, lg, NEG)
            lt_v[:, span] = lg
            top = jnp.maximum(top, lg)
        top = jnp.max(top, axis=1, keepdims=True)
        total = jnp.zeros((slots, rows), F32)
        for t in range(toks // rows):
            span = slice(t * rows, (t + 1) * rows)
            w = jnp.exp(lt_v[:, span] - top)
            total = total + w
            w_v[:, span] = w.astype(BF16)
        total = jnp.sum(total, axis=1, keepdims=True)
        sums = dot(w_v[...], x_v[q], 1, 0)
        stat = jnp.zeros((slots, 128), F32)
        for pos, val in ((0, top), (3, total)):
            rest = val
            for i in range(3):
                piece = rest.astype(BF16).astype(F32)
                rest = rest - piece
                stat = jnp.where(lane == pos + i, piece, stat)
        for k in range(2):
            dst = pl.ds(2 * q + k, chips, stride=2 * half)
            for d in range(dim // 128):
                pack_v[d, dst, :] = sums[k * chips:(k + 1) * chips, d * 128:(d + 1) * 128]
            pack_v[dim // 128, dst, :] = stat[k * chips:(k + 1) * chips, :]

    for d in range(dim // 128 + 1):
        send_v[:, :, d * 128:(d + 1) * 128] = pack_v[d].astype(BF16).reshape(chips, 2 * half, 128)
    recv_v[0] = send_v[chip]

    pl.semaphore_wait(barrier, chips)

    @pl.loop(1, chips)
    def _(r):
        to = peer(r)
        pltpu.make_async_remote_copy(send_v.at[to], recv_v.at[r], sems.at[0], sems.at[1], device_id={"seq": to}, device_id_type=MESH).start()

    def mix_weights(q):
        unit_rows(q)
        for t in range(toks // rows):
            span = slice(t * rows, (t + 1) * rows)
            lg = g * dot(u_v[span, :], v_v[...], 1, 0)
            e = jnp.exp(lg - jnp.max(lg, axis=1, keepdims=True))
            c_v[q, span, :] = (e / jnp.sum(e, axis=1, keepdims=True)).astype(BF16)
        pltpu.make_async_copy(c_v.at[q], c_hbm.at[batch_of(q)], c_sem).start()

    @pl.loop(0, half)
    def _(q):
        mix_weights(q)

    arrived = recv_v.at[pl.ds(1, chips - 1)]
    pltpu.make_async_copy(arrived, arrived, sems.at[1]).wait()
    n_rows = 2 * half
    got = recv_v[:, :, dim:].reshape(chips * n_rows, 128)
    sel_row = lax.broadcasted_iota(jnp.int32, (128, 128), 0)
    tops = dot(got, (sel_row < 3).astype(F32).astype(BF16), 1, 0).reshape(chips, n_rows, 128)
    totals = dot(got, ((sel_row >= 3) & (sel_row < 6)).astype(F32).astype(BF16), 1, 0).reshape(chips, n_rows, 128)
    factor = jnp.exp(tops - jnp.max(tops, axis=0, keepdims=True))
    z = jnp.sum(factor * totals, axis=0)
    for d in range(dim // 128):
        cols = slice(d * 128, (d + 1) * 128)
        acc = jnp.sum(factor * recv_v[:, :, cols].astype(F32), axis=0)
        xs_v[core, :, cols] = (acc / z).astype(BF16)

    def to_partner(src, dst, i):
        return pltpu.make_async_remote_copy(src, dst, sems.at[i], sems.at[i + 1], device_id={"model": other}, device_id_type=MESH)

    xs_copy = to_partner(xs_v.at[core], xs_v.at[core], 2)
    xs_copy.start()
    win_copy.wait()
    wout_copy.wait()
    xs_copy.wait()

    ins = xs_v[...].reshape(2 * n_rows, dim)
    parity = lax.broadcasted_iota(jnp.int32, (2 * n_rows, dim), 0) % 2
    out = None
    for k in range(2):
        hid = dot(ins, win_v[k], 1, 0)
        hid = (0.5 * hid * (1.0 + lax.erf(hid * 0.7071067811865476))).astype(BF16)
        res = dot(hid, wout_v[k], 1, 0)
        out = res if out is None else jnp.where(parity == k, res, out)
    part_v[...] = out.reshape(2, n_rows, dim)
    part_copy = to_partner(part_v.at[other], peer_v, 4)
    part_copy.start()
    part_copy.wait()
    ys_v[...] = (part_v[core] + peer_v[...]).astype(BF16)
    ag_v[0] = ys_v[...]

    @pl.loop(1, chips)
    def _(r):
        pltpu.make_async_remote_copy(ys_v, ag_v.at[r], sems.at[6], sems.at[7], device_id={"seq": peer(r)}, device_id_type=MESH).start()

    @pl.loop(half, n_batch)
    def _(q):
        x_copy(q).wait()
        mix_weights(q)

    arrived = ag_v.at[pl.ds(1, chips - 1)]
    pltpu.make_async_copy(arrived, arrived, sems.at[7]).wait()

    @pl.loop(0, chips)
    def _(s):
        sz, sy, sx = s // (SIDE * SIDE), (s // SIDE) % SIDE, s % SIDE
        r = ((cz - sz + SIDE) % SIDE) * (SIDE * SIDE) + ((cy - sy + SIDE) % SIDE) * SIDE + (cx - sx + SIDE) % SIDE
        for d in range(dim // 128):
            unpack_v[d, pl.ds(pl.multiple_of(s * n_rows, n_rows), n_rows), :] = ag_v[r, :, d * 128:(d + 1) * 128].astype(F32)

    for i in range(half):
        for k in range(2):
            for d in range(dim // 128):
                slots_v[i, k * chips:(k + 1) * chips, d * 128:(d + 1) * 128] = unpack_v[d, pl.ds(2 * i + k, chips, stride=n_rows), :].astype(BF16)

    mine = slots_hbm.at[pl.ds(first, half)]
    keep = pltpu.make_async_copy(slots_v, mine, s_sem)
    give = to_partner(slots_v, mine, 8)
    keep.start()
    give.start()
    sent = send_v.at[pl.ds(1, chips - 1)]
    pltpu.make_async_copy(sent, sent, sems.at[0]).wait()
    sent = ag_v.at[pl.ds(1, chips - 1)]
    pltpu.make_async_copy(sent, sent, sems.at[6]).wait()
    pltpu.make_async_copy(c_v, c_hbm, c_sem).wait()
    keep.wait()
    give.wait()


def mix_kernel(lens, c, slots, y):
    left = lens[pl.program_id(0)] - lax.axis_index("seq") * c.shape[1]
    rows = 256
    for t in range(c.shape[1] // rows):
        span = slice(t * rows, (t + 1) * rows)
        out = dot(c[0, span, :], slots[0], 1, 0)
        pos = lax.broadcasted_iota(jnp.int32, out.shape, 0) + t * rows
        y[0, span, :] = jnp.where(pos < left, out, 0.0).astype(BF16)


def solution(mesh):
    def local_layer(tokens, lengths, slot_params, logit_scale, w_in, w_out):
        n_batch, toks, dim = tokens.shape
        slots = slot_params.shape[1]
        chips, half = slots // 2, n_batch // 2
        n_rows = 2 * half
        smem = pl.BlockSpec(memory_space=pltpu.SMEM)
        vmem = pl.BlockSpec(memory_space=pltpu.VMEM)
        hbm = pl.BlockSpec(memory_space=pl.ANY)
        dma = pltpu.SemaphoreType.DMA
        weights, slot_out = pl.pallas_call(
            moe_kernel,
            name="moe",
            out_shape=(jax.ShapeDtypeStruct((n_batch, toks, slots), BF16), jax.ShapeDtypeStruct((n_batch, slots, dim), BF16)),
            in_specs=[smem, smem, vmem, hbm, hbm, hbm],
            out_specs=(hbm, hbm),
            scratch_shapes=[
                pltpu.VMEM((n_batch, toks, dim), BF16),
                pltpu.VMEM(w_in.shape, BF16),
                pltpu.VMEM(w_out.shape, BF16),
                pltpu.VMEM((n_batch, toks, slots), BF16),
                pltpu.VMEM((toks, dim), BF16),
                pltpu.VMEM((dim, slots), BF16),
                pltpu.VMEM((slots, dim), BF16),
                pltpu.VMEM((dim // 128, slots, 128), F32),
                pltpu.VMEM((slots, toks), F32),
                pltpu.VMEM((slots, toks), BF16),
                pltpu.VMEM((dim // 128 + 1, chips * n_rows, 128), F32),
                pltpu.VMEM((chips, n_rows, dim + 128), BF16),
                pltpu.VMEM((chips, n_rows, dim + 128), BF16),
                pltpu.VMEM((2, n_rows, dim), BF16),
                pltpu.VMEM((2, n_rows, dim), F32),
                pltpu.VMEM((n_rows, dim), F32),
                pltpu.VMEM((n_rows, dim), BF16),
                pltpu.VMEM((chips, n_rows, dim), BF16),
                pltpu.VMEM((dim // 128, chips * n_rows, 128), F32),
                pltpu.VMEM((half, slots, dim), BF16),
                dma((n_batch,)), dma((2,)), dma, dma, dma((10,)),
            ],
            compiler_params=pltpu.CompilerParams(collective_id=0, has_side_effects=True, vmem_limit_bytes=58 * 2**20),
        )(lengths, logit_scale.reshape(1), slot_params, tokens, w_in, w_out)
        return pl.pallas_call(
            mix_kernel,
            name="mix",
            out_shape=jax.ShapeDtypeStruct(tokens.shape, BF16),
            grid=(n_batch,),
            in_specs=[smem, pl.BlockSpec((1, toks, slots), lambda b: (b, 0, 0)), pl.BlockSpec((1, slots, dim), lambda b: (b, 0, 0))],
            out_specs=pl.BlockSpec((1, toks, dim), lambda b: (b, 0, 0)),
            compiler_params=pltpu.CompilerParams(dimension_semantics=("arbitrary",)),
        )(lengths, weights, slot_out)

    return jax.shard_map(local_layer, mesh=mesh, in_specs=(P("data", "seq", None), P("data"), P(), P(), P("seq", None, "model"), P("seq", "model", None)), out_specs=P("data", "seq", None), check_vma=False)
```

time: 780 us -> 48.1 us (0.06)
  the two profiles are of different devices: /device:TPU:2 before, /device:TPU:1 now
where the time goes in v1:
time: 48.1 us; the launch traced here: 47.8 us
  Pallas kernels  47.1 us (98%)
  between operations  0.66 us (1%)
    pallas_call x1, Pallas kernels, local_layer(): pl.pallas_call(moe_kernel, name='moe', out_shape=(jax.ShapeDtypeStruct((n...  38.2 us
    pallas_call x1, Pallas kernels, local_layer(): pl.pallas_call(mix_kernel, name='mix', out_shape=jax.ShapeDtypeStruct(tok...  8.88 us

profile of v1, /device:TPU:1, one launch (start us, length us, event | category | flops | bytes accessed | tf_op | source)
XLA Modules:
  0.0 47.8 jit_solution(12996574508172440596)
XLA Ops:
  0.7 38.2 %moe.1 = (bf16[8,1536,128]{2,1,0:T(8,128)(2,1)}, bf16[8,128,384]{2,1,0:T(8,128)(2,1)}) custom-call(s32[8]{0:T(128)} %lens.3, f32[1]{0:T(128)} %bitcast.1.scale, bf16[384,128]{1,0:T(8,128)(2,1)} %phi.1, bf16[8,1536,384]{2,1,0:T(8,128)(2,1)} %x_hbm.1, bf16[2,384,768]{2,1,0:T(8,128)(2,1)} %win_hbm.1, bf16[2,768,384]{2,1,0:T(8,128)(2,1)} %wout_hbm.1), custom_call_target="tpu_custom_call" | custom-call | tf_op jit(solution)/shard_map/moe/pallas_call | solution.py:235
  38.9 8.9 %mix.1 = bf16[8,1536,384]{2,1,0:T(8,128)(2,1)} custom-call(s32[8]{0:T(128)} %lens.3, bf16[8,1536,128]{2,1,0:T(8,128)(2,1)} %get-tuple-element.7.c, bf16[8,128,384]{2,1,0:T(8,128)(2,1)} %get-tuple-element.8.slots), custom_call_target="tpu_custom_call" | custom-call | tf_op jit(solution)/shard_map/mix/pallas_call | solution.py:266

commit v2 on v1

v2 whole, which is shorter than its diff:
```python
import jax
import jax.numpy as jnp
from jax import lax
from jax.experimental import pallas as pl
from jax.experimental.pallas import tpu as pltpu
from jax.sharding import PartitionSpec as P

NORM_EPS = 1e-6
MESH = pl.DeviceIdType.MESH
SIDE = 4
F32, BF16 = jnp.float32, jnp.bfloat16
NEG = -1e30
scope = jax.named_scope


def dot(a, b, ca, cb):
    return lax.dot_general(a, b, (((ca,), (cb,)), ((), ())), preferred_element_type=F32)


def far_first():
    near = (0, 1, 2, 1)
    every = [(z, y, x) for z in range(SIDE) for y in range(SIDE) for x in range(SIDE)]
    return sorted(every[1:], key=lambda o: (-sum(near[i] for i in o), o))


def moe_kernel(lens_hbm, scale, phi_hbm, x_hbm, win_hbm, wout_hbm, c_v, slots_v, left_v,
               lens, phi, x_v, win_v, wout_v, u_v, v_v, vt_v, tmp_v, lt_v, w_v, pack_v, send_v, recv_v,
               xs_v, part_v, peer_v, ys_v, ag_v, unpack_v,
               x_sem, l_sem, sems):
    n_batch, toks, dim = x_hbm.shape
    half = n_batch // 2
    slots = phi.shape[1]
    chips = slots // 2
    core = lax.axis_index("model")
    chip = lax.axis_index("seq")
    cz, cy, cx = chip // (SIDE * SIDE), (chip // SIDE) % SIDE, chip % SIDE
    first = core * half
    other = 1 - core

    def batch_of(q):
        return lax.rem(first + q, n_batch)

    def x_copy(q):
        return pltpu.make_async_copy(x_hbm.at[batch_of(q)], x_v.at[q], x_sem.at[q])

    loads = [pltpu.make_async_copy(a, b, l_sem.at[i]) for i, (a, b) in enumerate(
        ((phi_hbm, phi), (lens_hbm, lens), (win_hbm, win_v), (wout_hbm, wout_v)))]
    for load in loads[:2]:
        load.start()
    for q in range(n_batch):
        x_copy(q).start()
    for load in loads[2:]:
        load.start()

    at_z = [(cz + d) % SIDE * (SIDE * SIDE) for d in range(SIDE)]
    at_y = [(cy + d) % SIDE * SIDE for d in range(SIDE)]
    at_x = [(cx + d) % SIDE for d in range(SIDE)]
    peers = [at_z[z] + at_y[y] + at_x[x] for z, y, x in far_first()]

    with scope("signal"):
        barrier = pltpu.get_barrier_semaphore()
        for to in peers:
            pl.semaphore_signal(barrier, inc=1, device_id={"seq": to}, device_id_type=MESH)
        pl.semaphore_signal(barrier, inc=1, device_id={"model": other}, device_id_type=MESH)

    with scope("phi"):
        for load in loads[:2]:
            load.wait()
        g = scale[...]
        p32 = phi[...].astype(F32)
        unit = (p32 * lax.rsqrt(jnp.sum(p32 * p32, axis=0, keepdims=True) + NORM_EPS))
        for d in range(dim // 128):
            cols = slice(d * 128, (d + 1) * 128)
            tmp_v[d] = unit[cols, :].T
            for k in range(2):
                vt_v[k * chips:(k + 1) * chips, cols] = tmp_v[d, pl.ds(k, chips, stride=2), :].astype(BF16)
        v_v[...] = vt_v[...].astype(F32).T.astype(BF16)
        for b in range(n_batch):
            left_v[b:b + 1, :] = jnp.full((1, 128), lens[b] - chip * toks, jnp.int32)

    rows = 256

    def unit_rows(q):
        for t in range(toks // rows):
            part = x_v[q, t * rows:(t + 1) * rows, :].astype(F32)
            norm = lax.rsqrt(jnp.sum(part * part, axis=1, keepdims=True) + NORM_EPS)
            u_v[t * rows:(t + 1) * rows, :] = (part * norm).astype(BF16)

    lane = lax.broadcasted_iota(jnp.int32, (slots, 128), 1)

    def dispatch(q):
        x_copy(q).wait()
        unit_rows(q)
        left = lens[batch_of(q)] - chip * toks
        top = jnp.full((slots, rows), NEG, F32)
        for t in range(toks // rows):
            span = slice(t * rows, (t + 1) * rows)
            lg = g * dot(vt_v[...], u_v[span, :], 1, 1)
            pos = lax.broadcasted_iota(jnp.int32, lg.shape, 1) + t * rows
            lg = jnp.where(pos < left, lg, NEG)
            lt_v[:, span] = lg
            top = jnp.maximum(top, lg)
        top = jnp.max(top, axis=1, keepdims=True)
        total = jnp.zeros((slots, rows), F32)
        for t in range(toks // rows):
            span = slice(t * rows, (t + 1) * rows)
            w = jnp.exp(lt_v[:, span] - top)
            total = total + w
            w_v[:, span] = w.astype(BF16)
        total = jnp.sum(total, axis=1, keepdims=True)
        sums = dot(w_v[...], x_v[q], 1, 0)
        stat = jnp.zeros((slots, 128), F32)
        for pos, val in ((0, top), (3, total)):
            rest = val
            for i in range(3):
                piece = rest.astype(BF16).astype(F32)
                rest = rest - piece
                stat = jnp.where(lane == pos + i, piece, stat)
        for k in range(2):
            dst = pl.ds(2 * q + k, chips, stride=2 * half)
            for d in range(dim // 128):
                pack_v[d, dst, :] = sums[k * chips:(k + 1) * chips, d * 128:(d + 1) * 128]
            pack_v[dim // 128, dst, :] = stat[k * chips:(k + 1) * chips, :]

    with scope("dispatch"):
        @pl.loop(0, half)
        def _(q):
            dispatch(q)

    with scope("pack"):
        for d in range(dim // 128 + 1):
            send_v[:, :, d * 128:(d + 1) * 128] = pack_v[d].astype(BF16).reshape(chips, 2 * half, 128)
        recv_v[chip] = send_v[chip]

    with scope("barrier"):
        pl.semaphore_wait(barrier, chips)

    with scope("send"):
        for to in peers:
            pltpu.make_async_remote_copy(send_v.at[to], recv_v.at[chip], sems.at[0], sems.at[1], device_id={"seq": to}, device_id_type=MESH).start()

    def mix_weights(q):
        unit_rows(q)
        b = batch_of(q)
        for t in range(toks // rows):
            span = slice(t * rows, (t + 1) * rows)
            lg = g * dot(u_v[span, :], v_v[...], 1, 0)
            e = jnp.exp(lg - jnp.max(lg, axis=1, keepdims=True))
            c_v[b, span, :] = (e / jnp.sum(e, axis=1, keepdims=True)).astype(BF16)

    with scope("mix1"):
        @pl.loop(0, half)
        def _(q):
            mix_weights(q)

    with scope("wait_a2a"):
        arrived = recv_v.at[pl.ds(1, chips - 1)]
        pltpu.make_async_copy(arrived, arrived, sems.at[1]).wait()

    n_rows = 2 * half
    with scope("meet"):
        got = recv_v[:, :, dim:].reshape(chips * n_rows, 128)
        sel_row = lax.broadcasted_iota(jnp.int32, (128, 128), 0)
        tops = dot(got, (sel_row < 3).astype(F32).astype(BF16), 1, 0).reshape(chips, n_rows, 128)
        totals = dot(got, ((sel_row >= 3) & (sel_row < 6)).astype(F32).astype(BF16), 1, 0).reshape(chips, n_rows, 128)
        factor = jnp.exp(tops - jnp.max(tops, axis=0, keepdims=True))
        z = jnp.sum(factor * totals, axis=0)
        for d in range(dim // 128):
            cols = slice(d * 128, (d + 1) * 128)
            acc = jnp.sum(factor * recv_v[:, :, cols].astype(F32), axis=0)
            xs_v[core, :, cols] = (acc / z).astype(BF16)

    def to_partner(src, dst, i):
        return pltpu.make_async_remote_copy(src, dst, sems.at[i], sems.at[i + 1], device_id={"model": other}, device_id_type=MESH)

    with scope("xs_exchange"):
        xs_copy = to_partner(xs_v.at[core], xs_v.at[core], 2)
        xs_copy.start()
        for load in loads[2:]:
            load.wait()
        xs_copy.wait()

    with scope("ffn"):
        ins = xs_v[...].reshape(2 * n_rows, dim)
        parity = lax.broadcasted_iota(jnp.int32, (2 * n_rows, dim), 0) % 2
        out = None
        for k in range(2):
            hid = dot(ins, win_v[k], 1, 0)
            hid = (0.5 * hid * (1.0 + lax.erf(hid * 0.7071067811865476))).astype(BF16)
            res = dot(hid, wout_v[k], 1, 0)
            out = res if out is None else jnp.where(parity == k, res, out)
        part_v[...] = out.reshape(2, n_rows, dim)

    with scope("out_exchange"):
        part_copy = to_partner(part_v.at[other], peer_v, 4)
        part_copy.start()
        part_copy.wait()

    with scope("send2"):
        ys_v[...] = (part_v[core] + peer_v[...]).astype(BF16)
        ag_v[chip] = ys_v[...]
        for to in peers:
            pltpu.make_async_remote_copy(ys_v, ag_v.at[chip], sems.at[6], sems.at[7], device_id={"seq": to}, device_id_type=MESH).start()

    with scope("mix2"):
        @pl.loop(half, n_batch)
        def _(q):
            x_copy(q).wait()
            mix_weights(q)

    with scope("wait_ag"):
        arrived = ag_v.at[pl.ds(1, chips - 1)]
        pltpu.make_async_copy(arrived, arrived, sems.at[7]).wait()

    with scope("unpack"):
        for d in range(dim // 128):
            cols = slice(d * 128, (d + 1) * 128)
            unpack_v[d] = ag_v[:, :, cols].astype(F32).reshape(chips * n_rows, 128)
            for i in range(half):
                for k in range(2):
                    slots_v[first + i, k * chips:(k + 1) * chips, cols] = unpack_v[d, pl.ds(2 * i + k, chips, stride=n_rows), :].astype(BF16)

    with scope("finish"):
        mine = slots_v.at[pl.ds(first, half)]
        give = to_partner(mine, mine, 8)
        give.start()
        sent = send_v.at[pl.ds(1, chips - 1)]
        pltpu.make_async_copy(sent, sent, sems.at[0]).wait()
        sent = ag_v.at[pl.ds(1, chips - 1)]
        pltpu.make_async_copy(sent, sent, sems.at[6]).wait()
        give.wait()


def mix_kernel(left, c, slots, y_hbm, y_v, sem):
    n_batch, toks, _ = c.shape
    rows, parts = 256, 2

    def put(b, h):
        span = pl.ds(h * (toks // parts), toks // parts)
        return pltpu.make_async_copy(y_v.at[b, span], y_hbm.at[b, span], sem)

    @pl.loop(0, n_batch)
    def _(b):
        bound = jnp.broadcast_to(left[pl.ds(b, 1), :1], (rows, slots.shape[2]))
        for h in range(parts):
            for t in range(h * (toks // parts), (h + 1) * (toks // parts), rows):
                span = slice(t, t + rows)
                out = dot(c[b, span, :], slots[b], 1, 0)
                pos = lax.broadcasted_iota(jnp.int32, out.shape, 0) + t
                y_v[b, span, :] = jnp.where(pos < bound, out, 0.0).astype(BF16)
            put(b, h).start()

    pltpu.make_async_copy(y_v, y_hbm, sem).wait()


def solution(mesh):
    def local_layer(tokens, lengths, slot_params, logit_scale, w_in, w_out):
        n_batch, toks, dim = tokens.shape
        slots = slot_params.shape[1]
        chips, half = slots // 2, n_batch // 2
        n_rows = 2 * half
        vmem = pl.BlockSpec(memory_space=pltpu.VMEM)
        hbm = pl.BlockSpec(memory_space=pltpu.HBM)
        dma = pltpu.SemaphoreType.DMA
        weights, slot_out, left = pl.pallas_call(
            moe_kernel,
            name="moe",
            out_shape=(pltpu.VMEM((n_batch, toks, slots), BF16), pltpu.VMEM((n_batch, slots, dim), BF16), pltpu.VMEM((n_batch, 128), jnp.int32)),
            in_specs=[hbm, pl.BlockSpec(memory_space=pltpu.SMEM)] + [hbm] * 4,
            out_specs=(vmem, vmem, vmem),
            scratch_shapes=[
                pltpu.SMEM((n_batch,), jnp.int32),
                                pltpu.VMEM(slot_params.shape, BF16),
                pltpu.VMEM((n_batch, toks, dim), BF16),
                pltpu.VMEM(w_in.shape, BF16),
                pltpu.VMEM(w_out.shape, BF16),
                pltpu.VMEM((toks, dim), BF16),
                pltpu.VMEM((dim, slots), BF16),
                pltpu.VMEM((slots, dim), BF16),
                pltpu.VMEM((dim // 128, slots, 128), F32),
                pltpu.VMEM((slots, toks), F32),
                pltpu.VMEM((slots, toks), BF16),
                pltpu.VMEM((dim // 128 + 1, chips * n_rows, 128), F32),
                pltpu.VMEM((chips, n_rows, dim + 128), BF16),
                pltpu.VMEM((chips, n_rows, dim + 128), BF16),
                pltpu.VMEM((2, n_rows, dim), BF16),
                pltpu.VMEM((2, n_rows, dim), F32),
                pltpu.VMEM((n_rows, dim), F32),
                pltpu.VMEM((n_rows, dim), BF16),
                pltpu.VMEM((chips, n_rows, dim), BF16),
                pltpu.VMEM((dim // 128, chips * n_rows, 128), F32),
                dma((n_batch,)), dma((5,)), dma((10,)),
            ],
            compiler_params=pltpu.CompilerParams(collective_id=0, has_side_effects=True, vmem_limit_bytes=63100000),
        )(lengths, logit_scale, slot_params, tokens, w_in, w_out)
        return pl.pallas_call(
            mix_kernel,
            name="mix",
            out_shape=jax.ShapeDtypeStruct(tokens.shape, BF16),
            in_specs=[vmem, vmem, vmem],
            out_specs=hbm,
            scratch_shapes=[pltpu.VMEM(tokens.shape, BF16), dma],
            compiler_params=pltpu.CompilerParams(vmem_limit_bytes=20 * 2**20),
        )(left, weights, slot_out)

    return jax.shard_map(local_layer, mesh=mesh, in_specs=(P("data", "seq", None), P("data"), P(), P(), P("seq", None, "model"), P("seq", "model", None)), out_specs=P("data", "seq", None), check_vma=False)
```

time: 48.1 us -> 40.3 us (0.84)
  Pallas kernels: 47.1 us -> 39.5 us
    pallas_call x1, Pallas kernels: 8.88 us -> 4.57 us  [local_layer(): pl.pallas_call(mix_kernel, name='mix', out_shape=jax.ShapeDtypeStruct(tok...]
    pallas_call x1, Pallas kernels: 38.2 us -> 35 us  [local_layer(): pl.pallas_call(moe_kernel, name='moe', out_shape=(pltpu.VMEM((n_batch, to...]
where the time goes in v2:
time: 40.3 us; the launch traced here: 40.2 us
  Pallas kernels  39.5 us (98%)
  between operations  0.66 us (2%)
    pallas_call x1, Pallas kernels, local_layer(): pl.pallas_call(moe_kernel, name='moe', out_shape=(pltpu.VMEM((n_batch, to...  35 us
    pallas_call x1, Pallas kernels, local_layer(): pl.pallas_call(mix_kernel, name='mix', out_shape=jax.ShapeDtypeStruct(tok...  4.57 us

profile of v2, /device:TPU:1, one launch (start us, length us, event | category | flops | bytes accessed | tf_op | source)
XLA Modules:
  0.0 40.2 jit_solution(8295007511738739522)
XLA Ops:
  0.7 35.0 %moe.1 = (bf16[8,1536,128]{2,1,0:T(8,128)(2,1)S(1)}, bf16[8,128,384]{2,1,0:T(8,128)(2,1)S(1)}, s32[8,128]{1,0:T(8,128)S(1)}) custom-call(s32[8]{0:T(128)} %lens_hbm.1, f32[]{:T(128)S(6)} %copy.7.scale, bf16[384,128]{1,0:T(8,128)(2,1)} %phi_hbm.1, bf16[8,1536,384]{2,1,0:T(8,128)(2,1)} %x_hbm.1, bf16[2,384,768]{2,1,0:T(8,128)(2,1)} %win_hbm.1, ...), custom_call_target="tpu_custom_call" | custom-call | tf_op jit(solution)/shard_map/moe/pallas_call | solution.py:265
  35.6 4.6 %mix.1 = bf16[8,1536,384]{2,1,0:T(8,128)(2,1)} custom-call(s32[8,128]{1,0:T(8,128)S(1)} %get-tuple-element.8.left, bf16[8,1536,128]{2,1,0:T(8,128)(2,1)S(1)} %get-tuple-element.9.c, bf16[8,128,384]{2,1,0:T(8,128)(2,1)S(1)} %get-tuple-element.10.slots), custom_call_target="tpu_custom_call" | custom-call | tf_op jit(solution)/shard_map/mix/pallas_call | solution.py:296

commit v3 on v0

v3 whole, which is shorter than its diff:
```python
import jax
import jax.numpy as jnp
from jax import lax
from jax.experimental import pallas as pl
from jax.experimental.pallas import tpu as pltpu
from jax.sharding import PartitionSpec as P

NORM_EPS = 1e-6
MESH = pl.DeviceIdType.MESH
SIDE = 4
F32, BF16 = jnp.float32, jnp.bfloat16
NEG = -1e30
LOG2E = 1.4426950408889634
ROUNDS = 2
scope = jax.named_scope


def dot(a, b, ca, cb):
    return lax.dot_general(a, b, (((ca,), (cb,)), ((), ())), preferred_element_type=F32)


def far_first():
    near = (0, 1, 2, 1)
    every = [(z, y, x) for z in range(SIDE) for y in range(SIDE) for x in range(SIDE)]
    return sorted(every[1:], key=lambda o: (-sum(near[i] for i in o), o))


def mix_rows(c, slots, left, b, at, span):
    outs = jnp.concatenate([slots[0, at], slots[1, at]], axis=0)
    out = dot(c[b, span, :], outs, 1, 0)
    pos = lax.broadcasted_iota(jnp.int32, out.shape, 0) + span.start
    bound = jnp.broadcast_to(left[pl.ds(b, 1), :1], out.shape)
    return jnp.where(pos < bound, out, 0.0).astype(BF16)


def moe_kernel(lens_hbm, scale, phi_hbm, x_hbm, win_hbm, wout_hbm, c_v, slots_v, left_v, y_v,
               lens, phi, x_v, win_v, wout_v, u_v, v_v, vt_v, tmp_v, lt_v, w_v, pack_v, send_v, recv_v,
               xs_v, xin_v, xout_v, ys_v, ag_v, unpack_v,
               x_sem, l_sem, sems):
    n_batch, toks, dim = x_hbm.shape
    half = n_batch // 2
    per = half // ROUNDS
    slots = phi.shape[1]
    chips = slots // 2
    n_rows = 2 * per
    core = lax.axis_index("model")
    chip = lax.axis_index("seq")
    cz, cy, cx = chip // (SIDE * SIDE), (chip // SIDE) % SIDE, chip % SIDE
    first = core * half
    other = 1 - core

    def batch_of(q):
        return lax.rem(first + q, n_batch)

    def x_copy(q):
        return pltpu.make_async_copy(x_hbm.at[batch_of(q)], x_v.at[q], x_sem.at[q])

    loads = [pltpu.make_async_copy(a, b, l_sem.at[i]) for i, (a, b) in enumerate(
        ((phi_hbm, phi), (lens_hbm, lens), (win_hbm.at[core], win_v.at[core]), (wout_hbm.at[core], wout_v.at[core])))]

    def to_partner(src, dst, i, h):
        return pltpu.make_async_remote_copy(src, dst, sems.at[i, h], sems.at[i + 1, h], device_id={"model": other}, device_id_type=MESH)

    swaps = [to_partner(win_hbm.at[other], win_v.at[core], 4, 0), to_partner(wout_hbm.at[other], wout_v.at[core], 4, 1)]

    late = 8 * cz + 5 * cy + 4 * cx
    early = jnp.where(late <= 20, 1, 0)
    sums_first = per + (half - per) * early
    mix_first = early * jnp.where(late <= 4, 2, jnp.where(late <= 14, 1, 0))
    mix_between = mix_first + 2 * early
    mix_next = 3 + 4 * early
    for load in loads[:2]:
        load.start()
    for q in range(per):
        x_copy(q).start()

    at_z = [(cz + d) % SIDE * (SIDE * SIDE) for d in range(SIDE)]
    at_y = [(cy + d) % SIDE * SIDE for d in range(SIDE)]
    at_x = [(cx + d) % SIDE for d in range(SIDE)]
    peers = [at_z[z] + at_y[y] + at_x[x] for z, y, x in far_first()]

    with scope("signal"):
        barrier = pltpu.get_barrier_semaphore()
        for to in peers:
            pl.semaphore_signal(barrier, inc=1, device_id={"seq": to}, device_id_type=MESH)
        pl.semaphore_signal(barrier, inc=1, device_id={"model": other}, device_id_type=MESH)

    with scope("phi"):
        for load in loads[:2]:
            load.wait()
        for q in range(per, n_batch):
            x_copy(q).start()
        for load in loads[2:]:
            load.start()
        g = scale[...] * LOG2E
        p32 = phi[...].astype(F32)
        unit = (p32 * lax.rsqrt(jnp.sum(p32 * p32, axis=0, keepdims=True) + NORM_EPS))
        for d in range(dim // 128):
            cols = slice(d * 128, (d + 1) * 128)
            tmp_v[d] = unit[cols, :].T
            for k in range(2):
                vt_v[k * chips:(k + 1) * chips, cols] = tmp_v[d, pl.ds(k, chips, stride=2), :].astype(BF16)
        v_v[...] = vt_v[...].astype(F32).T.astype(BF16)
        for b in range(n_batch):
            left_v[b:b + 1, :] = jnp.full((1, 128), lens[b] - chip * toks, jnp.int32)

    def unit_rows(q, u, start, size):
        for t in range(start, start + size, 64):
            span = slice(t, t + 64)
            part = x_v[q, span, :].astype(F32)
            norm = lax.rsqrt(jnp.sum(part * part, axis=1, keepdims=True) + NORM_EPS)
            u[span, :] = (x_v[q, span, :].astype(F32) * norm).astype(BF16)

    rows = 256
    lane = lax.broadcasted_iota(jnp.int32, (slots, 128), 1)
    spans = [slice(t, t + rows) for t in range(0, toks, rows)]

    def dispatch(q):
        x_copy(q).wait()
        u, lt, w_b = u_v, lt_v, w_v
        h, i = q // per, q % per
        left = lens[batch_of(q)] - chip * toks
        bias = jnp.where(lax.broadcasted_iota(jnp.int32, (1, toks), 1) < left, 0.0, NEG)
        top = jnp.full((slots, rows), NEG, F32)
        for span in spans:
            unit_rows(q, u, span.start, rows)
            lg = g * dot(vt_v[...], u[span, :], 1, 1) + bias[:, span]
            lt[:, span] = lg
            top = jnp.maximum(top, lg)
        top = jnp.max(top, axis=1, keepdims=True)
        total = jnp.zeros((slots, rows), F32)
        for span in spans:
            w = jnp.exp2(lt[:, span] - top)
            total = total + w
            w_b[:, span] = w.astype(BF16)
        total = jnp.sum(total, axis=1, keepdims=True)
        sums = dot(w_b[...], x_v[q], 1, 0)
        stat = jnp.zeros((slots, 128), F32)
        for pos, val in ((0, top), (3, total)):
            rest = val
            for j in range(3):
                piece = rest.astype(BF16).astype(F32)
                rest = rest - piece
                stat = jnp.where(lane == pos + j, piece, stat)
        for k in range(2):
            dst = pl.ds(k * per + i, chips, stride=n_rows)
            for d in range(dim // 128):
                pack_v[h, d, dst, :] = sums[k * chips:(k + 1) * chips, d * 128:(d + 1) * 128]
            pack_v[h, dim // 128, dst, :] = stat[k * chips:(k + 1) * chips, :]

    def send_sums(h):
        for d in range(dim // 128 + 1):
            send_v[h, :, :, d * 128:(d + 1) * 128] = pack_v[h, d].astype(BF16).reshape(chips, n_rows, 128)
        recv_v[h, chip] = send_v[h, chip]
        for to in peers:
            pltpu.make_async_remote_copy(send_v.at[h, to], recv_v.at[h, chip], sems.at[0, h], sems.at[1, h], device_id={"seq": to}, device_id_type=MESH).start()

    def mix_weights(q):
        b = batch_of(q)
        for span in spans:
            unit_rows(q, u_v, span.start, rows)
            lg = g * dot(u_v[span, :], v_v[...], 1, 0)
            e = jnp.exp2(lg - jnp.max(lg, axis=1, keepdims=True))
            c_v[b, span, :] = (e / jnp.sum(e, axis=1, keepdims=True)).astype(BF16)

    def mix_span(name, lo, hi):
        with scope(name):
            @pl.loop(lo, hi)
            def _(q):
                mix_weights(q)

    with scope("dispatch"):
        @pl.loop(0, sums_first)
        def _(q):
            dispatch(q)
    mix_span("mix0", 0, mix_first)
    with scope("barrier"):
        pl.semaphore_wait(barrier, chips)
    with scope("send"):
        send_sums(0)
        for swap in swaps:
            swap.start()
    with scope("dispatch2"):
        @pl.loop(sums_first, half)
        def _(q):
            dispatch(q)
    mix_span("mix01", mix_first, mix_between)
    with scope("sendb"):
        send_sums(1)
    for q in range(half, n_batch):
        x_copy(q).wait()
    mix_span("mix1", mix_between, mix_next)

    def wait_bytes(ref, sem):
        pltpu.make_async_copy(ref, ref, sem).wait()

    sel_row = lax.broadcasted_iota(jnp.int32, (128, 128), 0)
    pick_top = (sel_row < 3).astype(F32).astype(BF16)
    pick_total = ((sel_row >= 3) & (sel_row < 6)).astype(F32).astype(BF16)

    for h in range(ROUNDS):
        with scope("wait_a2a"):
            wait_bytes(recv_v.at[h, pl.ds(1, chips - 1)], sems.at[1, h])
        with scope("meet"):
            got = recv_v[h, :, :, dim:].astype(F32).reshape(chips * n_rows, 128).astype(BF16)
            tops = dot(got, pick_top, 1, 0).reshape(chips, n_rows, 128)
            totals = dot(got, pick_total, 1, 0).reshape(chips, n_rows, 128)
            factor = jnp.exp2(tops - jnp.max(tops, axis=0, keepdims=True))
            z = jnp.sum(factor * totals, axis=0)
            for d in range(dim // 128):
                cols = slice(d * 128, (d + 1) * 128)
                acc = jnp.sum(factor * recv_v[h, :, :, cols].astype(F32), axis=0)
                xs_v[:, :, cols] = (acc / z).reshape(2, per, 128)
            xin_v[h, core] = xs_v[core].astype(BF16)
            xout_v[h] = xs_v[other].astype(BF16)
        with scope("xs_exchange"):
            xs_copy = to_partner(xout_v.at[h], xin_v.at[h, core], 2, h)
            xs_copy.start()
            if h == 0:
                for load in loads[2:] + swaps:
                    load.wait()
            xs_copy.wait()
        with scope("ffn"):
            ins = xin_v[h].astype(F32).reshape(n_rows, dim).astype(BF16)
            out = 0.0
            for m in range(2):
                hid = dot(ins, win_v[m], 1, 0)
                hid = (0.5 * hid * (1.0 + lax.erf(hid * 0.7071067811865476))).astype(BF16)
                out = out + dot(hid, wout_v[m], 1, 0)
            ys_v[h] = out.astype(BF16)
            ag_v[h, chip] = ys_v[h]
        with scope("send2"):
            for to in peers:
                pltpu.make_async_remote_copy(ys_v.at[h], ag_v.at[h, chip], sems.at[6, h], sems.at[7, h], device_id={"seq": to}, device_id_type=MESH).start()

    mix_span("mix2", mix_next, n_batch)

    gives = []

    def unpack(h):
        with scope("wait_ag"):
            wait_bytes(ag_v.at[h, pl.ds(1, chips - 1)], sems.at[7, h])
        with scope("unpack"):
            for d in range(dim // 128):
                cols = slice(d * 128, (d + 1) * 128)
                unpack_v[d] = ag_v[h, :, :, cols].astype(F32).reshape(chips * n_rows, 128)
                for r in range(n_rows):
                    slots_v[core, h * n_rows + r, :, cols] = unpack_v[d, pl.ds(r, chips, stride=n_rows), :].astype(BF16)
            mine = slots_v.at[core, pl.ds(h * n_rows, n_rows)]
            give = to_partner(mine, mine, 8, h)
            give.start()
            gives.append(give)

    def mix_early(lo, hi):
        with scope("mix_early"):
            @pl.loop(lo, hi)
            def _(j):
                for span in spans:
                    y_v[j, span, :] = mix_rows(c_v, slots_v, left_v, j // per * half + j % per, j, span)

    unpack(0)
    with scope("wait_give"):
        gives[0].wait()
    mix_early(0, n_rows // 2)
    unpack(1)
    mix_early(n_rows // 2, n_rows)

    with scope("finish"):
        for h in range(ROUNDS):
            wait_bytes(send_v.at[h, pl.ds(1, chips - 1)], sems.at[0, h])
            wait_bytes(ag_v.at[h, pl.ds(1, chips - 1)], sems.at[6, h])
        gives[1].wait()


def mix_kernel(left, c, slots, y_v, y_hbm, rest_v, sems):
    n_batch, toks, _ = c.shape
    done, half = y_v.shape[0], n_batch // 2
    per = half // ROUNDS
    rows, parts = 256, 2

    def batch_of(j, h):
        return j // per * half + h * per + j % per

    for j in range(done):
        pltpu.make_async_copy(y_v.at[j], y_hbm.at[batch_of(j, 0)], sems.at[0]).start()

    @pl.loop(0, done)
    def _(j):
        b = batch_of(j, 1)
        for p in range(parts):
            for t in range(p * (toks // parts), (p + 1) * (toks // parts), rows):
                span = slice(t, t + rows)
                rest_v[j, span, :] = mix_rows(c, slots, left, b, done + j, span)
            span = pl.ds(p * (toks // parts), toks // parts)
            pltpu.make_async_copy(rest_v.at[j, span], y_hbm.at[b, span], sems.at[1]).start()

    pltpu.make_async_copy(y_v, y_hbm.at[pl.ds(0, done)], sems.at[0]).wait()
    pltpu.make_async_copy(rest_v, y_hbm.at[pl.ds(0, done)], sems.at[1]).wait()


def solution(mesh):
    def local_layer(tokens, lengths, slot_params, logit_scale, w_in, w_out):
        n_batch, toks, dim = tokens.shape
        slots = slot_params.shape[1]
        chips, half = slots // 2, n_batch // 2
        per = half // ROUNDS
        n_rows = 2 * per
        vmem = pl.BlockSpec(memory_space=pltpu.VMEM)
        hbm = pl.BlockSpec(memory_space=pltpu.HBM)
        dma = pltpu.SemaphoreType.DMA
        weights, slot_out, left, mixed = pl.pallas_call(
            moe_kernel,
            name="moe",
            out_shape=(pltpu.VMEM((n_batch, toks, slots), BF16), pltpu.VMEM((2, n_batch, chips, dim), BF16), pltpu.VMEM((n_batch, 128), jnp.int32), pltpu.VMEM((half, toks, dim), BF16)),
            in_specs=[hbm, pl.BlockSpec(memory_space=pltpu.SMEM)] + [hbm] * 4,
            out_specs=(vmem, vmem, vmem, vmem),
            scratch_shapes=[
                pltpu.SMEM((n_batch,), jnp.int32),
                pltpu.VMEM(slot_params.shape, BF16),
                pltpu.VMEM((n_batch, toks, dim), BF16),
                pltpu.VMEM(w_in.shape, BF16),
                pltpu.VMEM(w_out.shape, BF16),
                pltpu.VMEM((toks, dim), BF16),
                pltpu.VMEM((dim, slots), BF16),
                pltpu.VMEM((slots, dim), BF16),
                pltpu.VMEM((dim // 128, slots, 128), F32),
                pltpu.VMEM((slots, toks), F32),
                pltpu.VMEM((slots, toks), BF16),
                pltpu.VMEM((ROUNDS, dim // 128 + 1, chips * n_rows, 128), F32),
                pltpu.VMEM((ROUNDS, chips, n_rows, dim + 128), BF16),
                pltpu.VMEM((ROUNDS, chips, n_rows, dim + 128), BF16),
                pltpu.VMEM((2, per, dim), F32),
                pltpu.VMEM((ROUNDS, 2, per, dim), BF16),
                pltpu.VMEM((ROUNDS, per, dim), BF16),
                pltpu.VMEM((ROUNDS, n_rows, dim), BF16),
                pltpu.VMEM((ROUNDS, chips, n_rows, dim), BF16),
                pltpu.VMEM((dim // 128, chips * n_rows, 128), F32),
                dma((n_batch,)), dma((4,)), dma((10, ROUNDS)),
            ],
            compiler_params=pltpu.CompilerParams(collective_id=0, has_side_effects=True, vmem_limit_bytes=58380000),
        )(lengths, logit_scale, slot_params, tokens, w_in, w_out)
        return pl.pallas_call(
            mix_kernel,
            name="mix",
            out_shape=jax.ShapeDtypeStruct(tokens.shape, BF16),
            in_specs=[vmem, vmem, vmem, vmem],
            out_specs=hbm,
            scratch_shapes=[pltpu.VMEM((half, toks, dim), BF16), dma((2,))],
            compiler_params=pltpu.CompilerParams(vmem_limit_bytes=20 * 2**20),
        )(left, weights, slot_out, mixed)

    return jax.shard_map(local_layer, mesh=mesh, in_specs=(P("data", "seq", None), P("data"), P(), P(), P("seq", None, "model"), P("seq", "model", None)), out_specs=P("data", "seq", None), check_vma=False)
```

time: 780 us -> 34.2 us (0.04)
  the two profiles are of different devices: /device:TPU:2 before, /device:TPU:1 now
where the time goes in v3:
time: 34.2 us; the launch traced here: 34 us
  Pallas kernels  33.4 us (98%)
  between operations  0.66 us (2%)
    pallas_call x1, Pallas kernels, local_layer(): pl.pallas_call(moe_kernel, name='moe', out_shape=(pltpu.VMEM((n_batch, to...  29.7 us
    pallas_call x1, Pallas kernels, local_layer(): pl.pallas_call(mix_kernel, name='mix', out_shape=jax.ShapeDtypeStruct(tok...  3.63 us

profile of v3, /device:TPU:1, one launch (start us, length us, event | category | flops | bytes accessed | tf_op | source)
XLA Modules:
  0.0 34.0 jit_solution(2849621261614726754)
XLA Ops:
  0.7 29.7 %moe.1 = (bf16[8,1536,128]{2,1,0:T(8,128)(2,1)S(1)}, bf16[2,8,64,384]{3,2,1,0:T(8,128)(2,1)S(1)}, s32[8,128]{1,0:T(8,128)S(1)}, bf16[4,1536,384]{2,1,0:T(8,128)(2,1)S(1)}) custom-call(s32[8]{0:T(128)} %lens_hbm.1, f32[]{:T(128)S(6)} %copy.7.scale, bf16[384,128]{1,0:T(8,128)(2,1)} %phi_hbm.1, bf16[8,1536,384]{2,1,0:T(8,128)(2,1)} %x_hbm.1, ...), custom_call_target="tpu_custom_call" | custom-call | tf_op jit(solution)/shard_map/moe/pallas_call | solution.py:311
  30.4 3.6 %mix.1 = bf16[8,1536,384]{2,1,0:T(8,128)(2,1)} custom-call(s32[8,128]{1,0:T(8,128)S(1)} %get-tuple-element.9.left, bf16[8,1536,128]{2,1,0:T(8,128)(2,1)S(1)} %get-tuple-element.10.c, bf16[2,8,64,384]{3,2,1,0:T(8,128)(2,1)S(1)} %get-tuple-element.11.slots, bf16[4,1536,384]{2,1,0:T(8,128)(2,1)S(1)} %get-tuple-element.12.y_v), custom_call_target="tpu_custom_call" | custom-call | tf_op jit(solution)/shard_map/mix/pallas_call | solution.py:342

commit v4 on v3

--- a/solution.py
+++ b/solution.py
@@ -12,6 +12,7 @@
 NEG = -1e30
 LOG2E = 1.4426950408889634
 ROUNDS = 2
+DIRECT = (0, 1, 4)
 scope = jax.named_scope
 
 
@@ -35,7 +36,7 @@
 
 def moe_kernel(lens_hbm, scale, phi_hbm, x_hbm, win_hbm, wout_hbm, c_v, slots_v, left_v, y_v,
                lens, phi, x_v, win_v, wout_v, u_v, v_v, vt_v, tmp_v, lt_v, w_v, pack_v, send_v, recv_v,
-               xs_v, xin_v, xout_v, ys_v, ag_v, unpack_v,
+               xs_v, xin_v, xout_v, ys_v, ag_v, agx_v, unpack_v,
                x_sem, l_sem, sems):
     n_batch, toks, dim = x_hbm.shape
     half = n_batch // 2
@@ -68,7 +69,7 @@
     sums_first = per + (half - per) * early
     mix_first = early * jnp.where(late <= 4, 2, jnp.where(late <= 14, 1, 0))
     mix_between = mix_first + 2 * early
-    mix_next = 3 + 4 * early
+    mix_next = jnp.where(early == 1, mix_between + 2, 3)
     for load in loads[:2]:
         load.start()
     for q in range(per):
@@ -79,11 +80,20 @@
     at_x = [(cx + d) % SIDE for d in range(SIDE)]
     peers = [at_z[z] + at_y[y] + at_x[x] for z, y, x in far_first()]
 
+    in_direct = sum((chip == e).astype(jnp.int32) for e in DIRECT)
+    gets_both = in_direct == 1
+
+    by_start = sorted(range(chips), key=lambda a: 8 * (a // 16) + 5 * (a // 4 % 4) + 4 * (a % 4))
     with scope("signal"):
         barrier = pltpu.get_barrier_semaphore()
-        for to in peers:
+        for to in [jnp.where(chip == a, by_start[-1], a) for a in by_start[:-1]]:
             pl.semaphore_signal(barrier, inc=1, device_id={"seq": to}, device_id_type=MESH)
         pl.semaphore_signal(barrier, inc=1, device_id={"model": other}, device_id_type=MESH)
+
+        @pl.when(gets_both)
+        def _():
+            for to in peers:
+                pl.semaphore_signal(barrier, inc=1, device_id={"model": other, "seq": to}, device_id_type=MESH)
 
     with scope("phi"):
         for load in loads[:2]:
@@ -148,11 +158,14 @@
                 pack_v[h, d, dst, :] = sums[k * chips:(k + 1) * chips, d * 128:(d + 1) * 128]
             pack_v[h, dim // 128, dst, :] = stat[k * chips:(k + 1) * chips, :]
 
+    def serve_first(which):
+        return [jnp.where(chip == which, peers[-1], which)] + [jnp.where(to == which, peers[-1], to) for to in peers[:-1]]
+
     def send_sums(h):
         for d in range(dim // 128 + 1):
             send_v[h, :, :, d * 128:(d + 1) * 128] = pack_v[h, d].astype(BF16).reshape(chips, n_rows, 128)
         recv_v[h, chip] = send_v[h, chip]
-        for to in peers:
+        for to in serve_first(chips - 1):
             pltpu.make_async_remote_copy(send_v.at[h, to], recv_v.at[h, chip], sems.at[0, h], sems.at[1, h], device_id={"seq": to}, device_id_type=MESH).start()
 
     def mix_weights(q):
@@ -175,7 +188,7 @@
             dispatch(q)
     mix_span("mix0", 0, mix_first)
     with scope("barrier"):
-        pl.semaphore_wait(barrier, chips)
+        pl.semaphore_wait(barrier, chips + len(DIRECT) - in_direct)
     with scope("send"):
         send_sums(0)
         for swap in swaps:
@@ -230,26 +243,44 @@
             ys_v[h] = out.astype(BF16)
             ag_v[h, chip] = ys_v[h]
         with scope("send2"):
-            for to in peers:
+            for e in DIRECT:
+                pltpu.make_async_remote_copy(ys_v.at[h], agx_v.at[h, chip], sems.at[10, h], sems.at[11, h], device_id={"model": other, "seq": e}, device_id_type=MESH).start()
+            for to in serve_first(0):
                 pltpu.make_async_remote_copy(ys_v.at[h], ag_v.at[h, chip], sems.at[6, h], sems.at[7, h], device_id={"seq": to}, device_id_type=MESH).start()
 
     mix_span("mix2", mix_next, n_batch)
 
     gives = []
+
+    def spread(src, parity, h):
+        for d in range(dim // 128):
+            cols = slice(d * 128, (d + 1) * 128)
+            unpack_v[d] = src[h, :, :, cols].astype(F32).reshape(chips * n_rows, 128)
+            for r in range(n_rows):
+                slots_v[parity, h * n_rows + r, :, cols] = unpack_v[d, pl.ds(r, chips, stride=n_rows), :].astype(BF16)
 
     def unpack(h):
         with scope("wait_ag"):
             wait_bytes(ag_v.at[h, pl.ds(1, chips - 1)], sems.at[7, h])
         with scope("unpack"):
-            for d in range(dim // 128):
-                cols = slice(d * 128, (d + 1) * 128)
-                unpack_v[d] = ag_v[h, :, :, cols].astype(F32).reshape(chips * n_rows, 128)
-                for r in range(n_rows):
-                    slots_v[core, h * n_rows + r, :, cols] = unpack_v[d, pl.ds(r, chips, stride=n_rows), :].astype(BF16)
+            spread(ag_v, core, h)
             mine = slots_v.at[core, pl.ds(h * n_rows, n_rows)]
             give = to_partner(mine, mine, 8, h)
-            give.start()
             gives.append(give)
+
+            @pl.when(jnp.logical_not(gets_both))
+            def _():
+                give.start()
+
+            @pl.when(gets_both)
+            def _():
+                wait_bytes(agx_v.at[h], sems.at[11, h])
+                spread(agx_v, other, h)
+
+    def settle(h):
+        @pl.when(jnp.logical_not(gets_both))
+        def _():
+            gives[h].wait()
 
     def mix_early(lo, hi):
         with scope("mix_early"):
@@ -260,16 +291,19 @@
 
     unpack(0)
     with scope("wait_give"):
-        gives[0].wait()
-    mix_early(0, n_rows // 2)
+        settle(0)
+    early_rows = jnp.where(gets_both, n_rows, n_rows // 2)
+    mix_early(0, early_rows)
     unpack(1)
-    mix_early(n_rows // 2, n_rows)
+    mix_early(early_rows, n_rows)
 
     with scope("finish"):
         for h in range(ROUNDS):
             wait_bytes(send_v.at[h, pl.ds(1, chips - 1)], sems.at[0, h])
             wait_bytes(ag_v.at[h, pl.ds(1, chips - 1)], sems.at[6, h])
-        gives[1].wait()
+
+            wait_bytes(agx_v.at[h, pl.ds(0, len(DIRECT))], sems.at[10, h])
+        settle(1)
 
 
 def mix_kernel(left, c, slots, y_v, y_hbm, rest_v, sems):
@@ -334,8 +368,9 @@
                 pltpu.VMEM((ROUNDS, per, dim), BF16),
                 pltpu.VMEM((ROUNDS, n_rows, dim), BF16),
                 pltpu.VMEM((ROUNDS, chips, n_rows, dim), BF16),
+                pltpu.VMEM((ROUNDS, chips, n_rows, dim), BF16),
                 pltpu.VMEM((dim // 128, chips * n_rows, 128), F32),
-                dma((n_batch,)), dma((4,)), dma((10, ROUNDS)),
+                dma((n_batch,)), dma((4,)), dma((12, ROUNDS)),
             ],
             compiler_params=pltpu.CompilerParams(collective_id=0, has_side_effects=True, vmem_limit_bytes=58380000),
         )(lengths, logit_scale, slot_params, tokens, w_in, w_out)

time: 34.2 us -> 32 us (0.936)
  Pallas kernels: 33.4 us -> 31.2 us
    pallas_call x1, Pallas kernels: 29.7 us -> 27.6 us  [local_layer(): pl.pallas_call(moe_kernel, name='moe', out_shape=(pltpu.VMEM((n_batch, to...]
where the time goes in v4:
time: 32 us; the launch traced here: 31.8 us
  Pallas kernels  31.2 us (98%)
  between operations  0.66 us (2%)
    pallas_call x1, Pallas kernels, local_layer(): pl.pallas_call(moe_kernel, name='moe', out_shape=(pltpu.VMEM((n_batch, to...  27.6 us
    pallas_call x1, Pallas kernels, local_layer(): pl.pallas_call(mix_kernel, name='mix', out_shape=jax.ShapeDtypeStruct(tok...  3.63 us

profile of v4, /device:TPU:1, one launch (start us, length us, event | category | flops | bytes accessed | tf_op | source)
XLA Modules:
  0.0 31.8 jit_solution(17995639536650073055)
XLA Ops:
  0.7 27.6 %moe.1 = (bf16[8,1536,128]{2,1,0:T(8,128)(2,1)S(1)}, bf16[2,8,64,384]{3,2,1,0:T(8,128)(2,1)S(1)}, s32[8,128]{1,0:T(8,128)S(1)}, bf16[4,1536,384]{2,1,0:T(8,128)(2,1)S(1)}) custom-call(s32[8]{0:T(128)} %lens_hbm.1, f32[]{:T(128)S(6)} %copy.7.scale, bf16[384,128]{1,0:T(8,128)(2,1)} %phi_hbm.1, bf16[8,1536,384]{2,1,0:T(8,128)(2,1)} %x_hbm.1, ...), custom_call_target="tpu_custom_call" | custom-call | tf_op jit(solution)/shard_map/moe/pallas_call | solution.py:345
  28.2 3.6 %mix.1 = bf16[8,1536,384]{2,1,0:T(8,128)(2,1)} custom-call(s32[8,128]{1,0:T(8,128)S(1)} %get-tuple-element.9.left, bf16[8,1536,128]{2,1,0:T(8,128)(2,1)S(1)} %get-tuple-element.10.c, bf16[2,8,64,384]{3,2,1,0:T(8,128)(2,1)S(1)} %get-tuple-element.11.slots, bf16[4,1536,384]{2,1,0:T(8,128)(2,1)S(1)} %get-tuple-element.12.y_v), custom_call_target="tpu_custom_call" | custom-call | tf_op jit(solution)/shard_map/mix/pallas_call | solution.py:377

commit v5 on v4

--- a/solution.py
+++ b/solution.py
@@ -37,7 +37,7 @@
 def moe_kernel(lens_hbm, scale, phi_hbm, x_hbm, win_hbm, wout_hbm, c_v, slots_v, left_v, y_v,
                lens, phi, x_v, win_v, wout_v, u_v, v_v, vt_v, tmp_v, lt_v, w_v, pack_v, send_v, recv_v,
                xs_v, xin_v, xout_v, ys_v, ag_v, agx_v, unpack_v,
-               x_sem, l_sem, sems):
+               x_sem, l_sem, send_sem, recv_sem):
     n_batch, toks, dim = x_hbm.shape
     half = n_batch // 2
     per = half // ROUNDS
@@ -50,25 +50,28 @@
     first = core * half
     other = 1 - core
 
+    def wait_bytes(ref, sem):
+        pltpu.make_async_copy(ref, ref, sem).wait()
+
     def batch_of(q):
         return lax.rem(first + q, n_batch)
 
     def x_copy(q):
-        return pltpu.make_async_copy(x_hbm.at[batch_of(q)], x_v.at[q], x_sem.at[q])
-
-    loads = [pltpu.make_async_copy(a, b, l_sem.at[i]) for i, (a, b) in enumerate(
+        return pltpu.make_async_copy(x_hbm.at[batch_of(q)], x_v.at[q], x_sem.at[0 if q == 0 else 1 if q < half else 2])
+
+    loads = [pltpu.make_async_copy(a, b, l_sem.at[min(i, 2)]) for i, (a, b) in enumerate(
         ((phi_hbm, phi), (lens_hbm, lens), (win_hbm.at[core], win_v.at[core]), (wout_hbm.at[core], wout_v.at[core])))]
 
     def to_partner(src, dst, i, h):
-        return pltpu.make_async_remote_copy(src, dst, sems.at[i, h], sems.at[i + 1, h], device_id={"model": other}, device_id_type=MESH)
-
-    swaps = [to_partner(win_hbm.at[other], win_v.at[core], 4, 0), to_partner(wout_hbm.at[other], wout_v.at[core], 4, 1)]
+        return pltpu.make_async_remote_copy(src, dst, send_sem.at[i], recv_sem.at[i, h], device_id={"model": other}, device_id_type=MESH)
+
+    swaps = [to_partner(win_hbm.at[other], win_v.at[core], 5, 0), to_partner(wout_hbm.at[other], wout_v.at[core], 5, 0)]
 
     late = 8 * cz + 5 * cy + 4 * cx
     early = jnp.where(late <= 20, 1, 0)
     sums_first = per + (half - per) * early
     mix_first = early * jnp.where(late <= 4, 2, jnp.where(late <= 14, 1, 0))
-    mix_between = mix_first + 2 * early
+    mix_between = mix_first + early * (2 - jnp.where(late <= 4, 1 - core, 0))
     mix_next = jnp.where(early == 1, mix_between + 2, 3)
     for load in loads[:2]:
         load.start()
@@ -126,7 +129,9 @@
     spans = [slice(t, t + rows) for t in range(0, toks, rows)]
 
     def dispatch(q):
-        x_copy(q).wait()
+        @pl.when(q == 1)
+        def _():
+            wait_bytes(x_v.at[pl.ds(1, half - 1)], x_sem.at[1])
         u, lt, w_b = u_v, lt_v, w_v
         h, i = q // per, q % per
         left = lens[batch_of(q)] - chip * toks
@@ -158,15 +163,19 @@
                 pack_v[h, d, dst, :] = sums[k * chips:(k + 1) * chips, d * 128:(d + 1) * 128]
             pack_v[h, dim // 128, dst, :] = stat[k * chips:(k + 1) * chips, :]
 
-    def serve_first(which):
-        return [jnp.where(chip == which, peers[-1], which)] + [jnp.where(to == which, peers[-1], to) for to in peers[:-1]]
+    def serve_first(*favoured):
+        order = list(peers)
+        for a in reversed(favoured):
+            last = order[-1]
+            order = [jnp.where(chip == a, last, a)] + [jnp.where(to == a, last, to) for to in order[:-1]]
+        return order
 
     def send_sums(h):
         for d in range(dim // 128 + 1):
             send_v[h, :, :, d * 128:(d + 1) * 128] = pack_v[h, d].astype(BF16).reshape(chips, n_rows, 128)
         recv_v[h, chip] = send_v[h, chip]
-        for to in serve_first(chips - 1):
-            pltpu.make_async_remote_copy(send_v.at[h, to], recv_v.at[h, chip], sems.at[0, h], sems.at[1, h], device_id={"seq": to}, device_id_type=MESH).start()
+        for to in serve_first(63):
+            pltpu.make_async_remote_copy(send_v.at[h, to], recv_v.at[h, chip], send_sem.at[0], recv_sem.at[0, h], device_id={"seq": to}, device_id_type=MESH).start()
 
     def mix_weights(q):
         b = batch_of(q)
@@ -183,6 +192,8 @@
                 mix_weights(q)
 
     with scope("dispatch"):
+        wait_bytes(x_v.at[0], x_sem.at[0])
+
         @pl.loop(0, sums_first)
         def _(q):
             dispatch(q)
@@ -200,12 +211,8 @@
     mix_span("mix01", mix_first, mix_between)
     with scope("sendb"):
         send_sums(1)
-    for q in range(half, n_batch):
-        x_copy(q).wait()
+    wait_bytes(x_v.at[pl.ds(half, n_batch - half)], x_sem.at[2])
     mix_span("mix1", mix_between, mix_next)
-
-    def wait_bytes(ref, sem):
-        pltpu.make_async_copy(ref, ref, sem).wait()
 
     sel_row = lax.broadcasted_iota(jnp.int32, (128, 128), 0)
     pick_top = (sel_row < 3).astype(F32).astype(BF16)
@@ -213,7 +220,7 @@
 
     for h in range(ROUNDS):
         with scope("wait_a2a"):
-            wait_bytes(recv_v.at[h, pl.ds(1, chips - 1)], sems.at[1, h])
+            wait_bytes(recv_v.at[h, pl.ds(1, chips - 1)], recv_sem.at[0, h])
         with scope("meet"):
             got = recv_v[h, :, :, dim:].astype(F32).reshape(chips * n_rows, 128).astype(BF16)
             tops = dot(got, pick_top, 1, 0).reshape(chips, n_rows, 128)
@@ -227,12 +234,12 @@
             xin_v[h, core] = xs_v[core].astype(BF16)
             xout_v[h] = xs_v[other].astype(BF16)
         with scope("xs_exchange"):
-            xs_copy = to_partner(xout_v.at[h], xin_v.at[h, core], 2, h)
+            xs_copy = to_partner(xout_v.at[h], xin_v.at[h, core], 1, h)
             xs_copy.start()
             if h == 0:
-                for load in loads[2:] + swaps:
-                    load.wait()
-            xs_copy.wait()
+                wait_bytes(win_v, l_sem.at[2])
+                wait_bytes(win_v, recv_sem.at[5, 0])
+            xs_copy.wait_recv()
         with scope("ffn"):
             ins = xin_v[h].astype(F32).reshape(n_rows, dim).astype(BF16)
             out = 0.0
@@ -244,9 +251,9 @@
             ag_v[h, chip] = ys_v[h]
         with scope("send2"):
             for e in DIRECT:
-                pltpu.make_async_remote_copy(ys_v.at[h], agx_v.at[h, chip], sems.at[10, h], sems.at[11, h], device_id={"model": other, "seq": e}, device_id_type=MESH).start()
+                pltpu.make_async_remote_copy(ys_v.at[h], agx_v.at[h, chip], send_sem.at[3], recv_sem.at[3, h], device_id={"model": other, "seq": e}, device_id_type=MESH).start()
             for to in serve_first(0):
-                pltpu.make_async_remote_copy(ys_v.at[h], ag_v.at[h, chip], sems.at[6, h], sems.at[7, h], device_id={"seq": to}, device_id_type=MESH).start()
+                pltpu.make_async_remote_copy(ys_v.at[h], ag_v.at[h, chip], send_sem.at[2], recv_sem.at[2, h], device_id={"seq": to}, device_id_type=MESH).start()
 
     mix_span("mix2", mix_next, n_batch)
 
@@ -261,11 +268,11 @@
 
     def unpack(h):
         with scope("wait_ag"):
-            wait_bytes(ag_v.at[h, pl.ds(1, chips - 1)], sems.at[7, h])
+            wait_bytes(ag_v.at[h, pl.ds(1, chips - 1)], recv_sem.at[2, h])
         with scope("unpack"):
             spread(ag_v, core, h)
             mine = slots_v.at[core, pl.ds(h * n_rows, n_rows)]
-            give = to_partner(mine, mine, 8, h)
+            give = to_partner(mine, mine, 4, h)
             gives.append(give)
 
             @pl.when(jnp.logical_not(gets_both))
@@ -274,13 +281,13 @@
 
             @pl.when(gets_both)
             def _():
-                wait_bytes(agx_v.at[h], sems.at[11, h])
+                wait_bytes(agx_v.at[h], recv_sem.at[3, h])
                 spread(agx_v, other, h)
 
     def settle(h):
         @pl.when(jnp.logical_not(gets_both))
         def _():
-            gives[h].wait()
+            gives[h].wait_recv()
 
     def mix_early(lo, hi):
         with scope("mix_early"):
@@ -298,11 +305,16 @@
     mix_early(early_rows, n_rows)
 
     with scope("finish"):
-        for h in range(ROUNDS):
-            wait_bytes(send_v.at[h, pl.ds(1, chips - 1)], sems.at[0, h])
-            wait_bytes(ag_v.at[h, pl.ds(1, chips - 1)], sems.at[6, h])
-
-            wait_bytes(agx_v.at[h, pl.ds(0, len(DIRECT))], sems.at[10, h])
+        wait_bytes(send_v.at[:, pl.ds(1, chips - 1)], send_sem.at[0])
+        wait_bytes(xout_v, send_sem.at[1])
+        wait_bytes(ag_v.at[:, pl.ds(1, chips - 1)], send_sem.at[2])
+        wait_bytes(agx_v.at[:, pl.ds(0, len(DIRECT))], send_sem.at[3])
+        wait_bytes(win_v, send_sem.at[5])
+
+        @pl.when(jnp.logical_not(gets_both))
+        def _():
+            wait_bytes(slots_v.at[core], send_sem.at[4])
+
         settle(1)
 
 
@@ -370,7 +382,7 @@
                 pltpu.VMEM((ROUNDS, chips, n_rows, dim), BF16),
                 pltpu.VMEM((ROUNDS, chips, n_rows, dim), BF16),
                 pltpu.VMEM((dim // 128, chips * n_rows, 128), F32),
-                dma((n_batch,)), dma((4,)), dma((12, ROUNDS)),
+                dma((3,)), dma((3,)), dma((6,)), dma((6, ROUNDS)),
             ],
             compiler_params=pltpu.CompilerParams(collective_id=0, has_side_effects=True, vmem_limit_bytes=58380000),
         )(lengths, logit_scale, slot_params, tokens, w_in, w_out)

time: 32 us -> 31.8 us (level)
  no operation moved by 1% of the time
where the time goes in v5:
time: 31.8 us; the launch traced here: 31.7 us
  Pallas kernels  31.1 us (98%)
  between operations  0.66 us (2%)
    pallas_call x1, Pallas kernels, local_layer(): pl.pallas_call(moe_kernel, name='moe', out_shape=(pltpu.VMEM((n_batch, to...  27.4 us
    pallas_call x1, Pallas kernels, local_layer(): pl.pallas_call(mix_kernel, name='mix', out_shape=jax.ShapeDtypeStruct(tok...  3.63 us

profile of v5, /device:TPU:1, one launch (start us, length us, event | category | flops | bytes accessed | tf_op | source)
XLA Modules:
  0.0 31.7 jit_solution(6499534701700325450)
XLA Ops:
  0.7 27.4 %moe.1 = (bf16[8,1536,128]{2,1,0:T(8,128)(2,1)S(1)}, bf16[2,8,64,384]{3,2,1,0:T(8,128)(2,1)S(1)}, s32[8,128]{1,0:T(8,128)S(1)}, bf16[4,1536,384]{2,1,0:T(8,128)(2,1)S(1)}) custom-call(s32[8]{0:T(128)} %lens_hbm.1, f32[]{:T(128)S(6)} %copy.7.scale, bf16[384,128]{1,0:T(8,128)(2,1)} %phi_hbm.1, bf16[8,1536,384]{2,1,0:T(8,128)(2,1)} %x_hbm.1, ...), custom_call_target="tpu_custom_call" | custom-call | tf_op jit(solution)/shard_map/moe/pallas_call | solution.py:357
  28.1 3.6 %mix.1 = bf16[8,1536,384]{2,1,0:T(8,128)(2,1)} custom-call(s32[8,128]{1,0:T(8,128)S(1)} %get-tuple-element.9.left, bf16[8,1536,128]{2,1,0:T(8,128)(2,1)S(1)} %get-tuple-element.10.c, bf16[2,8,64,384]{3,2,1,0:T(8,128)(2,1)S(1)} %get-tuple-element.11.slots, bf16[4,1536,384]{2,1,0:T(8,128)(2,1)S(1)} %get-tuple-element.12.y_v), custom_call_target="tpu_custom_call" | custom-call | tf_op jit(solution)/shard_map/mix/pallas_call | solution.py:389

commit v6 on v5

--- a/solution.py
+++ b/solution.py
@@ -78,11 +78,6 @@
     for q in range(per):
         x_copy(q).start()
 
-    at_z = [(cz + d) % SIDE * (SIDE * SIDE) for d in range(SIDE)]
-    at_y = [(cy + d) % SIDE * SIDE for d in range(SIDE)]
-    at_x = [(cx + d) % SIDE for d in range(SIDE)]
-    peers = [at_z[z] + at_y[y] + at_x[x] for z, y, x in far_first()]
-
     in_direct = sum((chip == e).astype(jnp.int32) for e in DIRECT)
     gets_both = in_direct == 1
 
@@ -95,8 +90,13 @@
 
         @pl.when(gets_both)
         def _():
-            for to in peers:
+            for to in [jnp.where(chip == a, by_start[-1], a) for a in by_start[:-1]]:
                 pl.semaphore_signal(barrier, inc=1, device_id={"model": other, "seq": to}, device_id_type=MESH)
+
+    at_z = [(cz + d) % SIDE * (SIDE * SIDE) for d in range(SIDE)]
+    at_y = [(cy + d) % SIDE * SIDE for d in range(SIDE)]
+    at_x = [(cx + d) % SIDE for d in range(SIDE)]
+    peers = [at_z[z] + at_y[y] + at_x[x] for z, y, x in far_first()]
 
     with scope("phi"):
         for load in loads[:2]:

time: 31.8 us -> 31.7 us (level)
  no operation moved by 1% of the time
where the time goes in v6:
time: 31.7 us; the launch traced here: 31.6 us
  Pallas kernels  30.9 us (97%)
  between operations  0.66 us (2%)
    pallas_call x1, Pallas kernels, local_layer(): pl.pallas_call(moe_kernel, name='moe', out_shape=(pltpu.VMEM((n_batch, to...  27.3 us
    pallas_call x1, Pallas kernels, local_layer(): pl.pallas_call(mix_kernel, name='mix', out_shape=jax.ShapeDtypeStruct(tok...  3.63 us

profile of v6, /device:TPU:1, one launch (start us, length us, event | category | flops | bytes accessed | tf_op | source)
XLA Modules:
  0.0 31.6 jit_solution(13820027492008449976)
XLA Ops:
  0.7 27.3 %moe.1 = (bf16[8,1536,128]{2,1,0:T(8,128)(2,1)S(1)}, bf16[2,8,64,384]{3,2,1,0:T(8,128)(2,1)S(1)}, s32[8,128]{1,0:T(8,128)S(1)}, bf16[4,1536,384]{2,1,0:T(8,128)(2,1)S(1)}) custom-call(s32[8]{0:T(128)} %lens_hbm.1, f32[]{:T(128)S(6)} %copy.7.scale, bf16[384,128]{1,0:T(8,128)(2,1)} %phi_hbm.1, bf16[8,1536,384]{2,1,0:T(8,128)(2,1)} %x_hbm.1, ...), custom_call_target="tpu_custom_call" | custom-call | tf_op jit(solution)/shard_map/moe/pallas_call | solution.py:357
  28.0 3.6 %mix.1 = bf16[8,1536,384]{2,1,0:T(8,128)(2,1)} custom-call(s32[8,128]{1,0:T(8,128)S(1)} %get-tuple-element.9.left, bf16[8,1536,128]{2,1,0:T(8,128)(2,1)S(1)} %get-tuple-element.10.c, bf16[2,8,64,384]{3,2,1,0:T(8,128)(2,1)S(1)} %get-tuple-element.11.slots, bf16[4,1536,384]{2,1,0:T(8,128)(2,1)S(1)} %get-tuple-element.12.y_v), custom_call_target="tpu_custom_call" | custom-call | tf_op jit(solution)/shard_map/mix/pallas_call | solution.py:389

commit v7 on v6

--- a/solution.py
+++ b/solution.py
@@ -250,10 +250,11 @@
             ys_v[h] = out.astype(BF16)
             ag_v[h, chip] = ys_v[h]
         with scope("send2"):
-            for e in DIRECT:
-                pltpu.make_async_remote_copy(ys_v.at[h], agx_v.at[h, chip], send_sem.at[3], recv_sem.at[3, h], device_id={"model": other, "seq": e}, device_id_type=MESH).start()
-            for to in serve_first(0):
+            for n, to in enumerate(serve_first(0)):
                 pltpu.make_async_remote_copy(ys_v.at[h], ag_v.at[h, chip], send_sem.at[2], recv_sem.at[2, h], device_id={"seq": to}, device_id_type=MESH).start()
+                if n == 0:
+                    for e in DIRECT:
+                        pltpu.make_async_remote_copy(ys_v.at[h], agx_v.at[h, chip], send_sem.at[3], recv_sem.at[3, h], device_id={"model": other, "seq": e}, device_id_type=MESH).start()
 
     mix_span("mix2", mix_next, n_batch)
 

time: 31.7 us -> 32.2 us (1.016)
  no operation moved by 1% of the time
where the time goes in v7:
time: 32.2 us; the launch traced here: 31.8 us
  Pallas kernels  31.1 us (97%)
  between operations  0.66 us (2%)
    pallas_call x1, Pallas kernels, local_layer(): pl.pallas_call(moe_kernel, name='moe', out_shape=(pltpu.VMEM((n_batch, to...  27.5 us
    pallas_call x1, Pallas kernels, local_layer(): pl.pallas_call(mix_kernel, name='mix', out_shape=jax.ShapeDtypeStruct(tok...  3.63 us

profile of v7, /device:TPU:1, one launch (start us, length us, event | category | flops | bytes accessed | tf_op | source)
XLA Modules:
  0.0 31.8 jit_solution(6194470452329827243)
XLA Ops:
  0.7 27.5 %moe.1 = (bf16[8,1536,128]{2,1,0:T(8,128)(2,1)S(1)}, bf16[2,8,64,384]{3,2,1,0:T(8,128)(2,1)S(1)}, s32[8,128]{1,0:T(8,128)S(1)}, bf16[4,1536,384]{2,1,0:T(8,128)(2,1)S(1)}) custom-call(s32[8]{0:T(128)} %lens_hbm.1, f32[]{:T(128)S(6)} %copy.7.scale, bf16[384,128]{1,0:T(8,128)(2,1)} %phi_hbm.1, bf16[8,1536,384]{2,1,0:T(8,128)(2,1)} %x_hbm.1, ...), custom_call_target="tpu_custom_call" | custom-call | tf_op jit(solution)/shard_map/moe/pallas_call | solution.py:358
  28.1 3.6 %mix.1 = bf16[8,1536,384]{2,1,0:T(8,128)(2,1)} custom-call(s32[8,128]{1,0:T(8,128)S(1)} %get-tuple-element.9.left, bf16[8,1536,128]{2,1,0:T(8,128)(2,1)S(1)} %get-tuple-element.10.c, bf16[2,8,64,384]{3,2,1,0:T(8,128)(2,1)S(1)} %get-tuple-element.11.slots, bf16[4,1536,384]{2,1,0:T(8,128)(2,1)S(1)} %get-tuple-element.12.y_v), custom_call_target="tpu_custom_call" | custom-call | tf_op jit(solution)/shard_map/mix/pallas_call | solution.py:390
